TPU v7x, 32 devices: a whole 2x2x4 slice. The times are simulated.
32 devices in a mesh: seq: 8 (over z, y), head: 4 (over x, core).
Axes of the slice: x: 2, y: 2, z: 4, core: 2. Of those that a mesh axis runs over, the one named last changes fastest.
Arguments:
- layer_in: bfloat16 [4096, 2048], P('seq', 'head'), may hold values from -6 to 6
- query_weight: bfloat16 [2048, 1024], P(None, 'head'), may hold values from -0.125 to 0.125
- key_weight: bfloat16 [2048, 1024], P(None, 'head'), may hold values from -0.125 to 0.125
- value_weight: bfloat16 [2048, 1024], P(None, 'head'), may hold values from -0.125 to 0.125
- gate_weight: bfloat16 [2048, 1024], P(None, 'head'), may hold values from -0.125 to 0.125
- beta_weight: bfloat16 [2048, 8], P(None, 'head'), may hold values from -0.125 to 0.125
- decay_weight: bfloat16 [2048, 8], P(None, 'head'), may hold values from -0.125 to 0.125
- conv_weight: float32 [4, 3, 1024], P(None, None, 'head'), may hold values from -3 to 3
- decay_log: float32 [8], P('head'), as said below
- beta_bias: float32 [8], P('head'), as said below
- decay_bias: float32 [8], P('head'), may hold values from -1 to 1
- norm_gain: float32 [128], replicated, may hold values from 0.1 to 1.9
- out_weight: bfloat16 [1024, 2048], P('head'), may hold values from -0.1875 to 0.1875
Outputs:
- layer_out: bfloat16 [4096, 2048], P('seq', 'head')
Inputs may be any that keep to these rules, and one draw needn't show every extreme that they name: decay_log lies between log(0.1 / 4096) and log(0.05). beta_bias lies between log(0.5 * 128 / 4096) and 1.
All inputs are finite; a program needn't handle non-finite values.
Results may differ from a plain program's by a relative error of at most 0.0049.
Values may be sent and summed in bfloat16 or wider, within the bound.
A program may use at most 128 MiB of HBM per device.

v0:
```python
import functools

import jax
import jax.numpy as jnp
from jax import lax
from jax.experimental import pallas as pl
from jax.experimental.pallas import tpu as pltpu
from jax.sharding import PartitionSpec as P

BLOCK = 128
PRIOR = 16
LANES = 128
GROUPS = 2
PER_GROUP = 2
MESH = pl.DeviceIdType.MESH
F32 = jnp.float32
BF16 = jnp.bfloat16
norm_floor = 0.0001


def bits_below(limit):
    found = []
    bit = limit // 2
    while bit:
        found.append(bit)
        bit //= 2
    return found


def low_bit(value):
    return value & -value


def meet(peers):
    barrier = pltpu.get_barrier_semaphore()
    expected = 0
    for present, device in peers:
        if present is True:
            pl.semaphore_signal(barrier, inc=1, device_id=device, device_id_type=MESH)
            expected = expected + 1
        else:

            @pl.when(present)
            def _():
                pl.semaphore_signal(barrier, inc=1, device_id=device, device_id_type=MESH)

            expected = expected + present.astype(jnp.int32)
    pl.semaphore_wait(barrier, expected)


def remote(source, target, send_sem, recv_sem, device):
    return pltpu.make_async_remote_copy(
        src_ref=source,
        dst_ref=target,
        send_sem=send_sem,
        recv_sem=recv_sem,
        device_id=device,
        device_id_type=MESH,
    )


def dot(left, right, contract=((1,), (0,))):
    return lax.dot_general(
        left.astype(BF16), right.astype(BF16), (contract, ((), ())), preferred_element_type=F32
    )


def split(value):
    high = value.astype(BF16)
    return high, (value - high.astype(F32)).astype(BF16)


def dot3(left, right, contract=((1,), (0,))):
    lh, ll = left if isinstance(left, tuple) else split(left)
    rh, rl = right if isinstance(right, tuple) else split(right)
    axis = contract[1][0]
    both = dot(jnp.concatenate([lh, lh], axis=1), jnp.concatenate([rh, rl], axis=axis), contract)
    return both + dot(ll, rh, contract)


def layer_kernel(
    seqs, n, heads,
    x_ref, wq, wk, wv, wg, beta_in, step_in, taps_in, rates_in, bias_in, shift_in, gain_in, w_ref,
    out_ref,
    w_all, w_flat, x_own, buf, prior, raw, local, reader, maps, slab,
    w_buf, pair_buf, go_buf, in_buf, hid,
    beta_ref, step_ref, taps, gain, rates, beta_bias, decay_bias,
    load_sem, small_sem, x_sem, x_send, x_recv, p_send, p_recv, own_sem, w_send, w_recv,
    pair_sem, chain_send, chain_recv, h_send, h_recv,
):
    seq = lax.axis_index("seq")
    me = lax.axis_index("head")
    tokens, feats = x_ref.shape
    width = wq.shape[1]
    dim = LANES
    blocks = tokens // BLOCK
    columns = out_ref.shape[1]
    sends_each = GROUPS * PER_GROUP
    rows = tokens // sends_each
    group_rows = tokens // GROUPS
    group_blocks = blocks // GROUPS
    bits = bits_below(n)

    loads = [pltpu.make_async_copy(x_ref, x_own, x_sem)]
    for i, w in enumerate((wq, wk, wv, wg)):
        loads.append(
            pltpu.make_async_copy(w, w_all.at[:, pl.ds(i * width, width)], load_sem.at[i])
        )
    smalls = [
        pltpu.make_async_copy(source, target, small_sem.at[i])
        for i, (source, target) in enumerate((
            (beta_in, beta_ref), (step_in, step_ref), (taps_in, taps), (gain_in, gain),
            (rates_in, rates), (bias_in, beta_bias), (shift_in, decay_bias),
        ))
    ]
    for load in loads + smalls:
        load.start()
    has_next = seq < seqs - 1
    has_before = seq > 0
    far_next = seq < seqs - 2
    far_before = seq >= 2
    odd = seq % 2
    is_odd = odd == 1
    mate = seq + 1 - 2 * odd
    peers = [(True, (seq, me ^ m)) for m in range(1, n)]
    peers += [(has_next, (seq + 1, me ^ m)) for m in range(n)]
    peers += [(has_before, (seq - 1, me ^ m)) for m in range(n)]
    peers += [(far_next, (seq + 2, me)), (far_before, (seq - 2, me))]
    meet(peers)

    def hop(m, bit, c):
        piece = pl.ds(c * rows, rows)
        source = x_ref.at[piece] if m == 0 else buf.at[m, piece]
        got = m | bit
        return remote(
            source, buf.at[got, piece], x_send.at[got, c], x_recv.at[got, c], (seq, me ^ bit)
        )

    tails = [
        remote(
            x_ref.at[pl.ds(tokens - PRIOR, PRIOR)],
            prior.at[m],
            p_send.at[m],
            p_recv.at[m],
            (seq + 1, me ^ m),
        )
        for m in range(n)
    ]

    @pl.when(has_next)
    def _():
        for tail in tails:
            tail.start()

    hops = {}
    for bit in bits:
        for c in range(sends_each):
            hops[bit, c] = hop(0, bit, c)
            hops[bit, c].start()
    for load in smalls:
        load.wait()
    w_flat[...] = jnp.zeros(w_flat.shape, F32)
    w_flat[pl.ds(0, heads), :] = beta_ref[...].astype(F32)
    w_flat[pl.ds(heads, heads), :] = step_ref[...].astype(F32)
    for i in range(w_flat.shape[1] // LANES):
        piece = pl.ds(i * LANES, LANES)
        w_all[piece, pl.ds(4 * width, LANES)] = w_flat[:, piece].T.astype(BF16)
    for load in loads:
        load.wait()

    def weights_of(m):
        start = pl.multiple_of((me ^ m) * feats, LANES)
        return w_all[pl.ds(start, feats), :]

    def arrive(m, c):
        hops[m, c].wait_recv()
        for bit in bits:
            if bit < low_bit(m):
                hops[m | bit, c] = hop(m, bit, c)
                hops[m | bit, c].start()

    def add(m, g):
        piece = pl.ds(g * group_rows, group_rows)
        here = pl.ds(PRIOR + g * group_rows, group_rows)
        values = x_own[piece, :] if m == 0 else buf[m, piece, :]
        term = jnp.dot(values, weights_of(m), preferred_element_type=F32)
        if m == 0:
            raw[here, :] = term
        else:
            raw[here, :] = raw[here, :] + term

    for g in range(GROUPS):
        add(0, g)
    for g in range(GROUPS):
        for c in range(g * PER_GROUP, (g + 1) * PER_GROUP):
            arrive(1, c)
        add(1, g)

    def add_prior():
        @pl.when(has_before)
        def _():
            total = jnp.zeros((PRIOR, raw.shape[1]), F32)
            for m in range(n):
                tails[m].wait_recv()
                total = total + jnp.dot(prior[m], weights_of(m), preferred_element_type=F32)
            raw[pl.ds(0, PRIOR), :] = total

        @pl.when(jnp.logical_not(has_before))
        def _():
            raw[pl.ds(0, PRIOR), :] = jnp.zeros((PRIOR, raw.shape[1]), F32)

    row = lax.broadcasted_iota(jnp.int32, (BLOCK, BLOCK), 0)
    col = lax.broadcasted_iota(jnp.int32, (BLOCK, BLOCK), 1)
    within = row >= col
    before = row > col
    eye = (row == col).astype(F32)
    lower = within.astype(F32)
    lane = lax.broadcasted_iota(jnp.int32, (1, LANES), 1)
    offset = jnp.zeros((1, LANES), F32)
    rate = jnp.zeros((1, LANES), F32)
    for h in range(heads):
        offset = jnp.where(lane == h, beta_bias[h], offset)
        offset = jnp.where(lane == heads + h, decay_bias[h], offset)
        rate = jnp.where(lane == heads + h, rates[h], rate)
    rate = -jnp.exp(rate)

    def mixed(kind, h, b):
        base = kind * width + h * dim
        start = PRIOR + b * BLOCK
        total = None
        for s in range(taps.shape[1]):
            tap = taps[kind, pl.ds(s, 1), pl.ds(h * dim, dim)]
            term = tap * raw[pl.ds(start - s, BLOCK), pl.ds(base, dim)]
            total = term if total is None else total + term
        return total * jax.nn.sigmoid(total)

    def unit(values):
        return values * lax.rsqrt(jnp.sum(values * values, axis=-1, keepdims=True) + 1.0)

    def block_terms(g, midway):
        pairs = [(b, h) for b in range(g * group_blocks, (g + 1) * group_blocks)
                 for h in range(heads)]
        betas, runs, acrosses = {}, {}, {}
        for b in range(g * group_blocks, (g + 1) * group_blocks):
            small = raw[pl.ds(PRIOR + b * BLOCK, BLOCK), pl.ds(4 * width, LANES)] + offset
            betas[b] = jax.nn.sigmoid(small)
            steps = rate * (jnp.maximum(small, 0.0) + jnp.log1p(jnp.exp(-jnp.abs(small))))
            runs[b] = jnp.dot(
                lower, steps, precision=lax.Precision.HIGHEST, preferred_element_type=F32
            )
            acrosses[b] = runs[b].T
        lows, mixes, sides, weighteds, reads, ends = [], [], [], [], [], []
        for b, h in pairs:
            q = unit(mixed(0, h, b))
            k = unit(mixed(1, h, b))
            v = mixed(2, h, b)
            beta = betas[b][:, h : h + 1]
            down = runs[b][:, heads + h : heads + h + 1]
            along = acrosses[b][heads + h : heads + h + 1, :]
            last = down[BLOCK - 1 : BLOCK, :]
            decay = jnp.where(within, jnp.exp(jnp.minimum(down - along, 0.0)), 0.0)
            grams = dot3(jnp.concatenate([q, k], axis=0), k, ((1,), (1,)))
            mixes.append(decay * grams[:BLOCK])
            lows.append(jnp.where(before, beta * decay * grams[BLOCK:], 0.0))
            growth = jnp.exp(down)
            sides.append(jnp.concatenate([beta * v, (beta * growth) * k], axis=1))
            weighteds.append((jnp.exp(last - down) * k).T)
            reads.append(growth * q)
            ends.append(jnp.exp(last))
        inverses = [eye - jnp.where((row // 2 == col // 2), low, 0.0) for low in lows]
        span = 2
        while span < BLOCK:
            linked = (row // (2 * span) == col // (2 * span)) & (row // span > col // span)
            shares = [split(inv) for inv in inverses]
            middles = [
                dot3(jnp.where(linked, low, 0.0), share) for low, share in zip(lows, shares)
            ]
            inverses = [
                inv - dot3(share, middle)
                for inv, share, middle in zip(inverses, shares, middles)
            ]
            span *= 2
        midway()
        solved = [split(dot3(inv, side)) for inv, side in zip(inverses, sides)]
        found = {}
        for i, (b, h) in enumerate(pairs):
            got = dot3(weighteds[i], solved[i])
            transit = ends[i] * eye - got[:, dim:]
            reader[h, b, pl.ds(BLOCK, dim), :] = transit.astype(BF16)
            maps[h, b] = got[:, :dim]
            found[b, h] = (transit, got[:, :dim])

        def outputs():
            for i, (b, h) in enumerate(pairs):
                got = dot3(mixes[i], solved[i])
                local[h, pl.ds(b * BLOCK, BLOCK), :] = got[:, :dim]
                reader[h, b, pl.ds(0, BLOCK), :] = (reads[i] - got[:, dim:]).astype(BF16)

        return found, outputs

    def columns_of(m):
        return pl.ds(pl.multiple_of((me ^ m) * columns, LANES), columns)

    own = pltpu.make_async_copy(w_ref.at[:, columns_of(0)], w_buf.at[0], own_sem)
    moves = {
        m: remote(
            w_ref.at[:, columns_of(m)], w_buf.at[m], w_send.at[m], w_recv.at[m], (seq, me ^ m)
        )
        for m in range(1, n)
    }
    far = sorted(range(2, n), key=lambda m: (-low_bit(m), m))
    joined = [None] * heads
    for g in range(GROUPS):
        mine = range(g * PER_GROUP, (g + 1) * PER_GROUP)
        for m in far:
            for c in mine:
                if (m, "in", c) not in hops:
                    arrive(m, c)
            add(m, g)
        if g == 0:
            add_prior()

        def midway():
            if g == 0:
                own.start()
                for m in far:
                    moves[m].start()
            if g + 1 < GROUPS:
                for m in far:
                    if low_bit(m) > 1:
                        c = (g + 1) * PER_GROUP
                        arrive(m, c)
                        hops[m, "in", c] = None

        found, outputs = block_terms(g, midway)
        for h in range(heads):
            for b in range(g * group_blocks, (g + 1) * group_blocks):
                transit, carried = found[b, h]
                if joined[h] is None:
                    joined[h] = jnp.concatenate([transit, carried], axis=1)
                else:
                    moved = dot3(transit, joined[h])
                    joined[h] = jnp.concatenate(
                        [moved[:, :dim], moved[:, dim:] + carried], axis=1
                    )
        if g + 1 < GROUPS:
            outputs()
        else:
            for h in range(heads):
                slab[h] = joined[h].astype(slab.dtype)

    swaps = [
        remote(slab.at[h], pair_buf.at[h], pair_sem.at[0, h], pair_sem.at[1, h], (mate, me))
        for h in range(heads)
    ]
    for swap in swaps:
        swap.start()
    moves[1].start()

    outputs()
    for h in range(heads):
        place = pl.ds(PRIOR, tokens), pl.ds(3 * width + h * dim, dim)
        gate = raw[place]
        raw[place] = gain[...] * (gate * jax.nn.sigmoid(gate))

    firsts, comps = [], []
    for h in range(heads):
        swaps[h].wait()
        here = slab[h].astype(F32)
        there = pair_buf[h].astype(F32)
        first = jnp.where(is_odd, there, here)
        second = jnp.where(is_odd, here, there)
        moved = dot(second[:, :dim], first)
        comps.append((moved[:, :dim], moved[:, dim:] + second[:, dim:]))
        firsts.append(first)
    sends = [
        remote(go_buf.at[h], in_buf.at[h], chain_send.at[h], chain_recv.at[h], (seq + 2, me))
        for h in range(heads)
    ]

    @pl.when(jnp.logical_not(far_before))
    def _():
        in_buf[...] = jnp.zeros(in_buf.shape, in_buf.dtype)

    for h in range(heads):

        @pl.when(far_before)
        def _():
            sends[h].wait_recv()

        @pl.when(far_next)
        def _():
            go_buf[h] = (dot(comps[h][0], in_buf[h]) + comps[h][1]).astype(go_buf.dtype)
            sends[h].start()

    states = []
    for h in range(heads):
        arrived = in_buf[h].astype(F32)
        later = dot(firsts[h][:, :dim], arrived) + firsts[h][:, dim:]
        states.append(jnp.where(is_odd, later, arrived))

    lifts = {}

    def lift(m, bit, b):
        got = m | bit
        return remote(
            hid.at[m, b], hid.at[got, b], h_send.at[got, b], h_recv.at[got, b], (seq, me ^ bit)
        )

    def forward(m, b):
        limit = n if m == 0 else low_bit(m)
        for bit in bits:
            if bit < limit:
                lifts[m | bit, b] = lift(m, bit, b)
                lifts[m | bit, b].start()

    for b in range(blocks):
        for h in range(heads):
            got = dot(reader[h, b], states[h])
            states[h] = got[BLOCK:] + maps[h, b]
            head_out = got[:BLOCK] + local[h, pl.ds(b * BLOCK, BLOCK), :]
            gate = raw[pl.ds(PRIOR + b * BLOCK, BLOCK), pl.ds(3 * width + h * dim, dim)]
            scaled = head_out * lax.rsqrt(
                jnp.mean(head_out * head_out, axis=-1, keepdims=True) + norm_floor
            )
            hid[0, b, :, pl.ds(h * dim, dim)] = (
                scaled * gate
            ).astype(BF16)
        forward(0, b)

    own.wait()
    for move in moves.values():
        move.wait()
    order = sorted(range(1, n), key=lambda m: (m != 1, -low_bit(m), m))
    for b in range(blocks):
        total = jnp.dot(hid[0, b], w_buf[0], preferred_element_type=F32)
        for m in order:
            lifts[m, b].wait_recv()
            forward(m, b)
            total = total + jnp.dot(hid[m, b], w_buf[m], preferred_element_type=F32)
        out_ref[pl.ds(b * BLOCK, BLOCK), :] = total.astype(BF16)

    for key, copy in hops.items():
        if copy is not None:
            copy.wait_send()
    for copy in lifts.values():
        copy.wait_send()

    @pl.when(has_next)
    def _():
        for tail in tails:
            tail.wait_send()

    @pl.when(far_next)
    def _():
        for send in sends:
            send.wait_send()


def on_device(
    seqs, n,
    layer_in, query_weight, key_weight, value_weight, gate_weight, beta_weight, decay_weight,
    conv_weight, decay_log, beta_bias, decay_bias, norm_gain, out_weight,
):
    tokens, feats = layer_in.shape
    model, width = query_weight.shape
    heads = beta_weight.shape[1]
    dim = width // heads
    blocks = tokens // BLOCK
    total_width = 4 * width + LANES
    columns = out_weight.shape[1] // n
    vmem = pl.BlockSpec(memory_space=pltpu.VMEM)
    anywhere = pl.BlockSpec(memory_space=pl.ANY)
    dma = pltpu.SemaphoreType.DMA
    sends_each = GROUPS * PER_GROUP
    wire = BF16 if seqs <= 8 else F32
    return pl.pallas_call(
        functools.partial(layer_kernel, seqs, n, heads),
        out_shape=pltpu.VMEM((tokens, columns), BF16),
        in_specs=[anywhere] * 13,
        out_specs=vmem,
        scratch_shapes=[
            pltpu.VMEM((model, total_width), BF16),
            pltpu.VMEM((LANES, model), F32),
            pltpu.VMEM((tokens, feats), BF16),
            pltpu.VMEM((n, tokens, feats), BF16),
            pltpu.VMEM((n, PRIOR, feats), BF16),
            pltpu.VMEM((PRIOR + tokens, total_width), F32),
            pltpu.VMEM((heads, tokens, dim), F32),
            pltpu.VMEM((heads, blocks, BLOCK + dim, dim), BF16),
            pltpu.VMEM((heads, blocks, dim, dim), F32),
            pltpu.VMEM((heads, dim, 2 * dim), wire),
            pltpu.VMEM((n, width, columns), BF16),
            pltpu.VMEM((heads, dim, 2 * dim), wire),
            pltpu.VMEM((heads, dim, dim), wire),
            pltpu.VMEM((heads, dim, dim), wire),
            pltpu.VMEM((n, blocks, BLOCK, width), BF16),
            pltpu.VMEM((heads, model), BF16),
            pltpu.VMEM((heads, model), BF16),
            pltpu.VMEM((conv_weight.shape[1], conv_weight.shape[0], width), F32),
            pltpu.VMEM((1, dim), F32),
            pltpu.SMEM((heads,), F32),
            pltpu.SMEM((heads,), F32),
            pltpu.SMEM((heads,), F32),
            dma((4,)),
            dma((7,)),
            dma(()),
            dma((n, sends_each)),
            dma((n, sends_each)),
            dma((n,)),
            dma((n,)),
            dma(()),
            dma((n,)),
            dma((n,)),
            dma((2, heads)),
            dma((heads,)),
            dma((heads,)),
            dma((n, blocks)),
            dma((n, blocks)),
        ],
        compiler_params=pltpu.CompilerParams(
            collective_id=0, has_side_effects=True, vmem_limit_bytes=60 * 1024 * 1024
        ),
    )(
        layer_in, query_weight, key_weight, value_weight, gate_weight,
        beta_weight.T, decay_weight.T, conv_weight.transpose(1, 0, 2),
        decay_log, beta_bias, decay_bias, norm_gain[None], out_weight,
    )


def solution(mesh):
    return jax.shard_map(
        functools.partial(on_device, mesh.shape["seq"], mesh.shape["head"]),
        mesh=mesh,
        in_specs=(
            P("seq", "head"),
            P(None, "head"),
            P(None, "head"),
            P(None, "head"),
            P(None, "head"),
            P(None, "head"),
            P(None, "head"),
            P(None, None, "head"),
            P("head"),
            P("head"),
            P("head"),
            P(),
            P("head", None),
        ),
        out_specs=P("seq", "head"),
        check_vma=False,
    )
```

profile of v0, /device:TPU:25, one launch (start us, length us, event | category | flops | bytes accessed | tf_op | source)
XLA Modules:
  0.0 46.5 jit_solution(10341289737267177906)
XLA Ops:
  0.0 45.7 %shard_map.127 = bf16[512,512]{1,0:T(8,128)(2,1)S(1)} custom-call(bf16[512,512]{1,0:T(8,128)(2,1)} %x_ref.1, bf16[2048,256]{1,0:T(8,128)(2,1)} %wq.1, bf16[2048,256]{1,0:T(8,128)(2,1)} %wk.1, bf16[2048,256]{1,0:T(8,128)(2,1)} %wv.1, bf16[2048,256]{1,0:T(8,128)(2,1)} %wg.1, bf16[2,2048]{1,0:T(2,128)(2,1)} %bitcast.5, bf16[2,2048]{1,0:T(2,128)(2,1)} %bitcast.6, ...), custom_call_target="tpu_custom_call" | custom-call | tf_op jit(solution)/shard_map/pallas_call | solution.py:477
  45.7 0.8 %copy.15 = bf16[512,512]{1,0:T(8,128)(2,1)} copy(bf16[512,512]{1,0:T(8,128)(2,1)S(1)} %shard_map.127) | data formatting | bytes 1048576
where the time goes:
time: 46.7 us; the launch traced here: 46.5 us
  Pallas kernels  45.7 us (98%)
  local copies, waits for them, and re-layouts  0.8 us (2%)
    pallas_call x1, Pallas kernels, on_device(): pl.pallas_call(functools.partial(layer_kernel, seqs, n, heads), out_shape...  45.7 us

commit v1 on v0

v1 whole, which is shorter than its diff:
```python
import functools

import jax
import jax.numpy as jnp
from jax import lax
from jax.experimental import pallas as pl
from jax.experimental.pallas import tpu as pltpu
from jax.sharding import PartitionSpec as P

BLOCK = 128
PRIOR = 8
LANES = 128
PIECE = 64
BASE = 8
MESH = pl.DeviceIdType.MESH
F32 = jnp.float32
BF16 = jnp.bfloat16
norm_floor = 0.0001


def bits_below(limit):
    found = []
    bit = limit // 2
    while bit:
        found.append(bit)
        bit //= 2
    return found


def low_bit(value):
    return value & -value


def rounds_of(seqs):
    found = []
    half = 2
    while half < seqs:
        found.append(half)
        half *= 2
    return found


def meet(peers):
    barrier = pltpu.get_barrier_semaphore()
    expected = 0
    for present, device in peers:
        if present is True:
            pl.semaphore_signal(barrier, inc=1, device_id=device, device_id_type=MESH)
            expected = expected + 1
        else:

            @pl.when(present)
            def _():
                pl.semaphore_signal(barrier, inc=1, device_id=device, device_id_type=MESH)

            expected = expected + present.astype(jnp.int32)
    pl.semaphore_wait(barrier, expected)


def remote(source, target, send_sem, recv_sem, device):
    return pltpu.make_async_remote_copy(
        src_ref=source,
        dst_ref=target,
        send_sem=send_sem,
        recv_sem=recv_sem,
        device_id=device,
        device_id_type=MESH,
    )


def dot(left, right, contract=((1,), (0,))):
    return lax.dot_general(
        left.astype(BF16), right.astype(BF16), (contract, ((), ())), preferred_element_type=F32
    )


def split(value):
    high = value.astype(BF16)
    return high, (value - high.astype(F32)).astype(BF16)


def dot3(left, right, contract=((1,), (0,))):
    lh, ll = left if isinstance(left, tuple) else split(left)
    rh, rl = right if isinstance(right, tuple) else split(right)
    axis = contract[1][0]
    both = dot(jnp.concatenate([lh, lh], axis=1), jnp.concatenate([rh, rl], axis=axis), contract)
    return both + dot(ll, rh, contract)


def layer_kernel(
    seqs, n, heads,
    x_ref, wq, wk, wv, wg, beta_in, step_in, taps_in, rates_in, bias_in, shift_in, gain_in, w_ref,
    out_ref,
    w_all, w_flat, spread, x_own, buf, prior, raw, local, reader,
    slab_a, slab_c, mate_a, mate_c, go_a, go_c, in_a, in_c, pre_a, pre_c,
    w_buf, hid,
    beta_ref, step_ref, taps, gain, rates, beta_bias, decay_bias,
    load_sem, small_sem, x_sem, x_send, x_recv, p_send, p_recv, own_sem, w_send, w_recv,
    v_send, v_recv, sa_send, sa_recv, sc_send, sc_recv, side_send, a_send, a_recv, c_send, c_recv,
    h_send, h_recv,
):
    seq = lax.axis_index("seq")
    me = lax.axis_index("head")
    tokens, feats = x_ref.shape
    width = wq.shape[1]
    dim = LANES
    blocks = tokens // BLOCK
    columns = out_ref.shape[1]
    pieces = tokens // PIECE
    per_block = BLOCK // PIECE
    main = 2 * width + LANES
    total_width = w_all.shape[1]
    q_at = main
    g_at = main + width
    bits = bits_below(n)

    own_load = pltpu.make_async_copy(x_ref, x_own, x_sem)
    own_load.start()
    loads = []
    for i, (w, at) in enumerate(((wk, 0), (wv, width), (wq, q_at), (wg, g_at))):
        loads.append(pltpu.make_async_copy(w, w_all.at[:, pl.ds(at, width)], load_sem.at[i]))
    smalls = [
        pltpu.make_async_copy(source, target, small_sem.at[i])
        for i, (source, target) in enumerate((
            (beta_in, beta_ref), (step_in, step_ref), (taps_in, taps), (gain_in, gain),
            (rates_in, rates), (bias_in, beta_bias), (shift_in, decay_bias),
        ))
    ]
    for load in smalls + loads:
        load.start()
    has_next = seq < seqs - 1
    has_before = seq > 0
    odd = seq % 2
    is_odd = odd == 1
    mate = seq + 1 - 2 * odd
    lone = heads // 2
    rounds = rounds_of(seqs)
    uppers, sources, origins, whole = [], [], [], []
    for half in rounds:
        inside = seq % (2 * half)
        uppers.append(inside >= half)
        sources.append(inside // 2 == half // 2 - 1)
        origins.append(seq - inside + half - 2 + odd)
        whole.append(seq - inside > 0)
    starts = seq == 1 if rounds else seq < 0
    gives_c = [seq >= 0 if h < lone else seq != 1 for h in range(heads)]
    gives_a = [seq != 0 if h < lone else seq >= 2 for h in range(heads)]
    takes_c = [seq >= 0 if h < lone else seq != 0 for h in range(heads)]
    takes_a = [seq != 1 if h < lone else seq >= 2 for h in range(heads)]
    peers = [(True, (seq, me ^ m)) for m in range(1, n)]
    peers += [(has_next, (seq + 1, me ^ m)) for m in range(n)]
    peers += [(has_before, (seq - 1, me ^ m)) for m in range(n)]
    for r, half in enumerate(rounds):
        peers += [(sources[r], (seq + 2 + 2 * j, me)) for j in range(half // 2)]
        peers += [(uppers[r], (origins[r], me))]
    meet(peers)
    own_load.wait()

    def hop(m, bit, c):
        piece = pl.ds(c * PIECE, PIECE)
        source = x_own.at[piece] if m == 0 else buf.at[m, piece]
        got = m | bit
        return remote(
            source, buf.at[got, piece], x_send.at[got, c], x_recv.at[got, c], (seq, me ^ bit)
        )

    tails = [
        remote(
            x_own.at[pl.ds(tokens - PRIOR, PRIOR)],
            prior.at[m],
            p_send.at[m],
            p_recv.at[m],
            (seq + 1, me ^ m),
        )
        for m in range(n)
    ]

    @pl.when(has_next)
    def _():
        for tail in tails:
            tail.start()

    hops = {}
    for c in range(pieces):
        for bit in bits:
            hops[bit, c] = hop(0, bit, c)
            hops[bit, c].start()

    row = lax.broadcasted_iota(jnp.int32, (BLOCK, BLOCK), 0)
    col = lax.broadcasted_iota(jnp.int32, (BLOCK, BLOCK), 1)
    for j in range(BASE - 1):
        spread[:, pl.ds(j * LANES, LANES)] = (row == col // BASE * BASE + j).astype(F32).astype(BF16)

    for load in smalls:
        load.wait()
    w_flat[...] = jnp.zeros(w_flat.shape, F32)
    w_flat[pl.ds(0, heads), :] = beta_ref[...].astype(F32)
    w_flat[pl.ds(heads, heads), :] = step_ref[...].astype(F32)
    for i in range(w_flat.shape[1] // LANES):
        piece = pl.ds(i * LANES, LANES)
        w_all[piece, pl.ds(2 * width, LANES)] = w_flat[:, piece].T.astype(BF16)
    for load in loads:
        load.wait()

    def weights_of(m, cols):
        start = pl.multiple_of((me ^ m) * feats, LANES)
        return w_all[pl.ds(start, feats), cols]

    def arrive(m, c):
        hops[m, c].wait_recv()
        for bit in bits:
            if bit < low_bit(m):
                hops[m | bit, c] = hop(m, bit, c)
                hops[m | bit, c].start()

    every = pl.ds(0, total_width)
    first_cols = pl.ds(0, main)
    rest_cols = pl.ds(main, total_width - main)

    def add(ms, at, count, cols):
        here = pl.ds(PRIOR + at, count)
        total = None
        for m in ms:
            values = x_own[pl.ds(at, count), :] if m == 0 else buf[m, pl.ds(at, count), :]
            term = jnp.dot(values, weights_of(m, cols), preferred_element_type=F32)
            total = term if total is None else total + term
        if 0 not in ms:
            total = total + raw[here, cols]
        raw[here, cols] = total

    near = [m for m in range(1, n) if m == 1]
    far = sorted(range(2, n), key=lambda m: (-low_bit(m), m))
    step = 2 * BLOCK if tokens % (2 * BLOCK) == 0 else BLOCK
    for at in range(0, tokens, step):
        add([0], at, step, every)
    for at in range(0, tokens, step):
        for m in near:
            for c in range(at // PIECE, (at + step) // PIECE):
                arrive(m, c)
            add([m], at, step, every)

    within = row >= col
    before = row > col
    eye = (row == col).astype(F32)
    lower = within.astype(F32).astype(BF16)
    lower3 = jnp.concatenate([lower, lower, lower], axis=1)
    lane = lax.broadcasted_iota(jnp.int32, (1, LANES), 1)
    offset = jnp.zeros((1, LANES), F32)
    rate = jnp.zeros((1, LANES), F32)
    for h in range(heads):
        offset = jnp.where(lane == h, beta_bias[h], offset)
        offset = jnp.where(lane == heads + h, decay_bias[h], offset)
        rate = jnp.where(lane == heads + h, rates[h], rate)
    rate = -jnp.exp(rate)
    tiles = BLOCK // BASE
    tile_shape = (tiles, BASE, BLOCK)
    on_tile = (
        lax.broadcasted_iota(jnp.int32, tile_shape, 0)
        == lax.broadcasted_iota(jnp.int32, tile_shape, 2) // BASE
    )
    small_eye = (
        lax.broadcasted_iota(jnp.int32, (BASE, BLOCK), 0)
        == lax.broadcasted_iota(jnp.int32, (BASE, BLOCK), 1) % BASE
    ).astype(F32)

    def add_prior():
        @pl.when(has_before)
        def _():
            total = jnp.zeros((PRIOR, total_width), F32)
            for m in range(n):
                tails[m].wait_recv()
                total = total + jnp.dot(prior[m], weights_of(m, every), preferred_element_type=F32)
            raw[pl.ds(0, PRIOR), :] = total

        @pl.when(jnp.logical_not(has_before))
        def _():
            raw[pl.ds(0, PRIOR), :] = jnp.zeros((PRIOR, total_width), F32)

    def mixed(kind, h, b):
        base = (q_at, 0, width)[kind] + h * dim
        start = PRIOR + b * BLOCK
        total = None
        for s in range(taps.shape[1]):
            tap = taps[kind, pl.ds(s, 1), pl.ds(h * dim, dim)]
            term = tap * raw[pl.ds(start - s, BLOCK), pl.ds(base, dim)]
            total = term if total is None else total + term
        return total * jax.nn.sigmoid(total)

    def unit(values):
        return values * lax.rsqrt(jnp.sum(values * values, axis=-1, keepdims=True) + 1.0)

    def bases(lows):
        stack = []
        for low in lows:
            packed = jnp.sum(jnp.where(on_tile, low.reshape(tile_shape), 0.0), axis=0)
            high = packed.astype(BF16).astype(F32)
            stack += [high, packed - high]
        found = dot(jnp.concatenate(stack, axis=0), spread[...])
        results = []
        for h in range(len(lows)):
            inverse = small_eye
            for j in range(BASE - 1):
                cols = slice(j * LANES, (j + 1) * LANES)
                at = 2 * BASE * h
                factor = found[at : at + BASE, cols] + found[at + BASE : at + 2 * BASE, cols]
                inverse = inverse - factor * inverse[j : j + 1, :]
            results.append(
                jnp.where(on_tile, inverse[None], 0.0).reshape(BLOCK, BLOCK)
            )
        return results

    def small_terms(b):
        small = raw[pl.ds(PRIOR + b * BLOCK, BLOCK), pl.ds(2 * width, LANES)] + offset
        betas = jax.nn.sigmoid(small)
        steps = rate * (jnp.maximum(small, 0.0) + jnp.log1p(jnp.exp(-jnp.abs(small))))
        one, rest = split(steps)
        left = steps - one.astype(F32) - rest.astype(F32)
        run = dot(lower3, jnp.concatenate([one, rest, left.astype(BF16)], axis=0))
        return betas, run, run.T

    def block_terms(b, before_slab, midway):
        betas, run, across = small_terms(b)
        keys, decays, growths, lows, weighteds, ends = [], [], [], [], [], []
        sides = []
        for h in range(heads):
            k = unit(mixed(1, h, b))
            down = run[:, heads + h : heads + h + 1]
            along = across[heads + h : heads + h + 1, :]
            beta = betas[:, h : h + 1]
            last = down[BLOCK - 1 : BLOCK, :]
            decay = jnp.where(within, jnp.exp(jnp.minimum(down - along, 0.0)), 0.0)
            key = split(k)
            gram = dot3(key, key, ((1,), (1,)))
            lows.append(jnp.where(before, beta * decay * gram, 0.0))
            keys.append(key)
            decays.append(decay)
            growth = jnp.exp(down)
            growths.append(growth)
            ends.append(jnp.exp(last))
            weighteds.append((jnp.exp(last - down) * k).T)
        inverses = bases(lows)
        for h in range(heads):
            beta = betas[:, h : h + 1]
            v = mixed(2, h, b)
            scale = beta * growths[h]
            if before_slab is None:
                k = keys[h][0].astype(F32) + keys[h][1].astype(F32)
                sides.append(jnp.concatenate([-scale * k, beta * v], axis=1))
            else:
                moved = -scale * dot3(keys[h], before_slab[h])
                sides.append(
                    jnp.concatenate([moved[:, :dim], moved[:, dim:] + beta * v], axis=1)
                )
        span = BASE
        while 4 * span < BLOCK:
            area = (row // (4 * span) == col // (4 * span)) & (row // span > col // span)
            shares = [split(inv) for inv in inverses]
            links = [
                split(dot3(share, jnp.where(area, low, 0.0))) for share, low in zip(shares, lows)
            ]
            nexts = []
            for inv, share, link in zip(inverses, shares, links):
                pair = dot3(link, tuple(
                    jnp.concatenate([a, c], axis=1) for a, c in zip(share, link)
                ))
                nexts.append((inv - pair[:, :BLOCK], pair[:, BLOCK:]))
            inverses = [z + dot3(square, z) for z, square in nexts]
            span *= 4
        midway()
        area = row // span > col // span
        wide = [
            dot3(inv, jnp.concatenate([jnp.where(area, low, 0.0), side], axis=1))
            for inv, low, side in zip(inverses, lows, sides)
        ]
        links = [split(got[:, :BLOCK]) for got in wide]
        solved = [got[:, BLOCK:] for got in wide]
        level = span
        while level < BLOCK:
            nexts = []
            for link, have in zip(links, solved):
                share = split(have)
                more = level * 2 < BLOCK
                right = tuple(
                    jnp.concatenate([a, c], axis=1) for a, c in zip(share, link)
                ) if more else share
                got = dot3(link, right)
                nexts.append((got[:, : 2 * dim], got[:, 2 * dim :] if more else None))
            sign = -1.0 if level == span else 1.0
            solved = [have + sign * got for have, (got, _) in zip(solved, nexts)]
            links = [split(square) if square is not None else None for _, square in nexts]
            level *= 2
        slabs = []
        shares = [split(have) for have in solved]
        for h in range(heads):
            got = dot3(weighteds[h], shares[h])
            if before_slab is None:
                slabs.append(jnp.concatenate([ends[h] * eye + got[:, :dim], got[:, dim:]], axis=1))
            else:
                high, rest = before_slab[h]
                have = high.astype(F32) + rest.astype(F32)
                slabs.append(ends[h] * have + got)

        def outputs():
            for h in range(heads):
                q = unit(mixed(0, h, b))
                mix = decays[h] * dot3(q, keys[h], ((1,), (1,)))
                lead = growths[h] * q
                if before_slab is None:
                    got = dot3(mix, shares[h])
                    read, here = got[:, :dim] + lead, got[:, dim:]
                else:
                    right = tuple(
                        jnp.concatenate([a, c], axis=0)
                        for a, c in zip(shares[h], before_slab[h])
                    )
                    got = dot3(jnp.concatenate([mix, lead], axis=1), right)
                    read, here = got[:, :dim], got[:, dim:]
                reader[h, b] = read.astype(BF16)
                local[h, b] = here

        return slabs, outputs

    def columns_of(m):
        return pl.ds(pl.multiple_of((me ^ m) * columns, LANES), columns)

    own = pltpu.make_async_copy(w_ref.at[:, columns_of(0)], w_buf.at[0], own_sem)
    share = width // 2

    def part_of(which):
        return pl.ds(pl.multiple_of(which * share, share), share)

    moves, passes = {}, {}
    for m in range(1, n):
        if m in near:
            source, target = w_ref.at[:, columns_of(m)], w_buf.at[m]
        else:
            source, target = w_ref.at[part_of(odd), columns_of(m)], w_buf.at[m, part_of(odd)]
            passes[m] = remote(
                w_buf.at[m, part_of(odd)], w_buf.at[m, part_of(odd)], v_send.at[m], v_recv.at[m],
                (mate, me),
            )
        moves[m] = remote(source, target, w_send.at[m], w_recv.at[m], (seq, me ^ m))

    def arrive_block(b):
        for c in range(b * per_block, (b + 1) * per_block):
            for m in far:
                if low_bit(m) > 1:
                    arrive(m, c)

    direct = [m for m in far if low_bit(m) > 1]
    passed = [m for m in far if low_bit(m) == 1]
    slabs = None
    outputs = []
    add_prior()
    arrive_block(0)
    add(direct, 0, BLOCK, first_cols)
    for b in range(blocks):
        for m in passed:
            for c in range(b * per_block, (b + 1) * per_block):
                arrive(m, c)
        add(passed, b * BLOCK, BLOCK, first_cols)

        def midway():
            if b + 1 < blocks:
                arrive_block(b + 1)
                add(direct, (b + 1) * BLOCK, BLOCK, first_cols)
            if b + 2 == max(blocks, 2):
                own.start()
                for m in far + near:
                    moves[m].start()

        prior_slab = None if slabs is None else [split(value) for value in slabs]
        slabs, later = block_terms(b, prior_slab, midway)
        outputs.append(later)

    swaps_a, swaps_c = [], []
    for h in range(heads):
        slab_c[h] = slabs[h][:, dim:].astype(slab_c.dtype)
        slab_a[h] = slabs[h][:, :dim].astype(slab_a.dtype)
        swaps_a.append(
            remote(slab_a.at[h], mate_a.at[h], sa_send.at[h], sa_recv.at[h], (mate, me))
        )
        swaps_c.append(
            remote(slab_c.at[h], mate_c.at[h], sc_send.at[h], sc_recv.at[h], (mate, me))
        )
    for h in range(heads):

        @pl.when(gives_c[h])
        def _():
            swaps_c[h].start()

        @pl.when(gives_a[h])
        def _():
            swaps_a[h].start()

    blank = jnp.zeros((dim, dim), slab_a.dtype)
    for h in range(heads):

        @pl.when(jnp.logical_not(takes_a[h]))
        def _():
            mate_a[h] = blank

        @pl.when(jnp.logical_not(takes_c[h]))
        def _():
            mate_c[h] = blank
        pre_c[h] = jnp.zeros((dim, dim), F32)

    for at in range(0, tokens, step):
        add(far, at, step, rest_cols)
    for h in range(heads):
        place = pl.ds(PRIOR, tokens), pl.ds(g_at + h * dim, dim)
        gate = raw[place]
        raw[place] = gain[...] * (gate * jax.nn.sigmoid(gate))
    for later in outputs:
        later()

    def total_copy(source, target, send_sem, recv_sem, r, h, j):
        return remote(
            source.at[r, h], target.at[r, h], send_sem.at[r, h, j], recv_sem.at[r, h],
            (seq + 2 + 2 * j, me),
        )

    totals_c, totals_a = {}, {}
    for r, half in enumerate(rounds):
        for h in range(heads):
            for j in range(half // 2):
                totals_c[r, h, j] = total_copy(go_c, in_c, c_send, c_recv, r, h, j)
                totals_a[r, h, j] = total_copy(go_a, in_a, a_send, a_recv, r, h, j)
    asides = {
        h: remote(go_c.at[0, h], in_c.at[0, h], side_send.at[h], c_recv.at[0, h], (seq + 1, me))
        for h in range(lone, heads) if rounds
    }
    pair_a, pair_c, firsts = [], [], []

    def giver(r, h):
        return sources[r] & (seq != 0) if r == 0 and h >= lone else sources[r]

    def send_total(r, h):
        @pl.when(giver(r, h))
        def _():
            total = pair_c[h] if r == 0 else dot(pair_a[h], pre_c[h]) + pair_c[h]
            go_c[r, h] = total.astype(go_c.dtype)
            for j in reversed(range(rounds[r] // 2)):
                totals_c[r, h, j].start()

            @pl.when(whole[r])
            def _():
                total = pair_a[h] if r == 0 else dot(pair_a[h], pre_a[h])
                go_a[r, h] = total.astype(go_a.dtype)
                for j in reversed(range(rounds[r] // 2)):
                    totals_a[r, h, j].start()

        if r == 0 and h in asides:

            @pl.when(starts)
            def _():
                asides[h].start()

    def take_total(r, h):
        first = seq % rounds[r] < 2

        @pl.when(uppers[r])
        def _():
            totals_c[r, h, 0].wait_recv()

            @pl.when(first)
            def _():
                pre_c[h] = in_c[r, h].astype(F32)

            @pl.when(jnp.logical_not(first))
            def _():
                pre_c[h] = dot(pre_a[h], in_c[r, h]) + pre_c[h]

            @pl.when(whole[r])
            def _():
                totals_a[r, h, 0].wait_recv()

                @pl.when(first)
                def _():
                    pre_a[h] = in_a[r, h].astype(F32)

                @pl.when(jnp.logical_not(first))
                def _():
                    pre_a[h] = dot(pre_a[h], in_a[r, h])

    def hand_over():
        for m in passes:
            moves[m].wait_recv()
            passes[m].start()

    lifts = {}

    def lift(m, bit, h, b):
        got = m | bit
        return remote(
            hid.at[m, h, b], hid.at[got, h, b],
            h_send.at[got, h, b], h_recv.at[got, h, b], (seq, me ^ bit),
        )

    def forward(m, h, b):
        limit = n if m == 0 else low_bit(m)
        for bit in bits:
            if bit < limit:
                lifts[m | bit, h, b] = lift(m, bit, h, b)
                lifts[m | bit, h, b].start()

    states = []

    def read(h, b):
        head_out = dot(reader[h, b], states[h]) + local[h, b]
        gate = raw[pl.ds(PRIOR + b * BLOCK, BLOCK), pl.ds(g_at + h * dim, dim)]
        scaled = head_out * lax.rsqrt(
            jnp.mean(head_out * head_out, axis=-1, keepdims=True) + norm_floor
        )
        hid[0, h, b] = (scaled * gate).astype(BF16)
        forward(0, h, b)

    for h in range(heads):
        @pl.when(takes_c[h])
        def _():
            swaps_c[h].wait_recv()

        @pl.when(takes_a[h])
        def _():
            swaps_a[h].wait_recv()

        here_a, here_c = slab_a[h].astype(F32), slab_c[h].astype(F32)
        there_a, there_c = mate_a[h].astype(F32), mate_c[h].astype(F32)
        left = jnp.where(is_odd, here_a, there_a)
        right_a = jnp.where(is_odd, there_a, here_a)
        right_c = jnp.where(is_odd, there_c, here_c)
        back_c = jnp.where(is_odd, here_c, there_c)
        moved = dot(left, jnp.concatenate([right_a, right_c], axis=1))
        pair_a.append(moved[:, :dim])
        pair_c.append(moved[:, dim:] + back_c)
        firsts.append((right_a, right_c))
        if rounds:
            send_total(0, h)

    upper = uppers[-1] if rounds else seq < 0

    @pl.when(upper)
    def _():
        hand_over()

    for r in range(len(rounds) - 1):
        for h in range(heads):
            take_total(r, h)
            send_total(r + 1, h)

    for h in range(heads):
        if rounds:
            take_total(len(rounds) - 1, h)
        first_a, first_c = firsts[h]
        state = pre_c[h]
        states.append(jnp.where(is_odd, dot(first_a, state) + first_c, state))
        if h + 1 < heads:
            for b in range(blocks // 2):
                read(h, b)

    @pl.when(jnp.logical_not(upper))
    def _():
        hand_over()

    for b in range(blocks):
        for h in range(heads):
            if h + 1 == heads or b >= blocks // 2:
                read(h, b)

    own.wait()
    for m in near:
        moves[m].wait_recv()
    order = sorted(range(1, n), key=lambda m: (m != 1, -low_bit(m), m))

    def rows_of(m, b):
        return jnp.concatenate([hid[m, h, b] for h in range(heads)], axis=1)

    for b in range(blocks):
        total = jnp.dot(rows_of(0, b), w_buf[0], preferred_element_type=F32)
        for m in order:
            if b == 0 and m in passes:
                passes[m].wait_recv()
            for h in range(heads):
                lifts[m, h, b].wait_recv()
                forward(m, h, b)
            total = total + jnp.dot(rows_of(m, b), w_buf[m], preferred_element_type=F32)
        out_ref[pl.ds(b * BLOCK, BLOCK), :] = total.astype(BF16)

    for copies in (hops, lifts, moves, passes):
        for copy in copies.values():
            copy.wait_send()

    for h in range(heads):

        @pl.when(gives_c[h])
        def _():
            swaps_c[h].wait_send()

        @pl.when(gives_a[h])
        def _():
            swaps_a[h].wait_send()

        if h in asides:

            @pl.when(starts)
            def _():
                asides[h].wait_send()

        for r, half in enumerate(rounds):

            @pl.when(giver(r, h))
            def _():
                for j in range(half // 2):
                    totals_c[r, h, j].wait_send()

                @pl.when(whole[r])
                def _():
                    for j in range(half // 2):
                        totals_a[r, h, j].wait_send()

    @pl.when(has_next)
    def _():
        for tail in tails:
            tail.wait_send()


def on_device(
    seqs, n,
    layer_in, query_weight, key_weight, value_weight, gate_weight, beta_weight, decay_weight,
    conv_weight, decay_log, beta_bias, decay_bias, norm_gain, out_weight,
):
    tokens, feats = layer_in.shape
    model, width = query_weight.shape
    heads = beta_weight.shape[1]
    dim = width // heads
    blocks = tokens // BLOCK
    pieces = tokens // PIECE
    total_width = 4 * width + LANES
    columns = out_weight.shape[1] // n
    vmem = pl.BlockSpec(memory_space=pltpu.VMEM)
    anywhere = pl.BlockSpec(memory_space=pl.ANY)
    dma = pltpu.SemaphoreType.DMA
    wire = BF16 if seqs <= 8 else F32
    steps = max(1, len(rounds_of(seqs)))
    most = max(1, seqs // 4)
    square = pltpu.VMEM((heads, dim, dim), wire)
    stage = pltpu.VMEM((steps, heads, dim, dim), wire)
    total = pltpu.VMEM((heads, dim, dim), F32)
    return pl.pallas_call(
        functools.partial(layer_kernel, seqs, n, heads),
        out_shape=pltpu.VMEM((tokens, columns), BF16),
        in_specs=[anywhere] * 13,
        out_specs=vmem,
        scratch_shapes=[
            pltpu.VMEM((model, total_width), BF16),
            pltpu.VMEM((LANES, model), F32),
            pltpu.VMEM((LANES, (BASE - 1) * LANES), BF16),
            pltpu.VMEM((tokens, feats), BF16),
            pltpu.VMEM((n, tokens, feats), BF16),
            pltpu.VMEM((n, PRIOR, feats), BF16),
            pltpu.VMEM((PRIOR + tokens, total_width), F32),
            pltpu.VMEM((heads, blocks, BLOCK, dim), F32),
            pltpu.VMEM((heads, blocks, BLOCK, dim), BF16),
            square, square, square, square,
            stage, stage, stage, stage,
            total, total,
            pltpu.VMEM((n, width, columns), BF16),
            pltpu.VMEM((n, heads, blocks, BLOCK, dim), BF16),
            pltpu.VMEM((heads, model), BF16),
            pltpu.VMEM((heads, model), BF16),
            pltpu.VMEM((conv_weight.shape[1], conv_weight.shape[0], width), F32),
            pltpu.VMEM((1, dim), F32),
            pltpu.SMEM((heads,), F32),
            pltpu.SMEM((heads,), F32),
            pltpu.SMEM((heads,), F32),
            dma((4,)),
            dma((7,)),
            dma(()),
            dma((n, pieces)),
            dma((n, pieces)),
            dma((n,)),
            dma((n,)),
            dma(()),
            dma((n,)),
            dma((n,)),
            dma((n,)),
            dma((n,)),
            dma((heads,)),
            dma((heads,)),
            dma((heads,)),
            dma((heads,)),
            dma((heads,)),
            dma((steps, heads, most)),
            dma((steps, heads)),
            dma((steps, heads, most)),
            dma((steps, heads)),
            dma((n, heads, blocks)),
            dma((n, heads, blocks)),
        ],
        compiler_params=pltpu.CompilerParams(
            collective_id=0, has_side_effects=True, vmem_limit_bytes=60 * 1024 * 1024
        ),
    )(
        layer_in, query_weight, key_weight, value_weight, gate_weight,
        beta_weight.T, decay_weight.T, conv_weight.transpose(1, 0, 2),
        decay_log, beta_bias, decay_bias, norm_gain[None], out_weight,
    )


def solution(mesh):
    return jax.shard_map(
        functools.partial(on_device, mesh.shape["seq"], mesh.shape["head"]),
        mesh=mesh,
        in_specs=(
            P("seq", "head"),
            P(None, "head"),
            P(None, "head"),
            P(None, "head"),
            P(None, "head"),
            P(None, "head"),
            P(None, "head"),
            P(None, None, "head"),
            P("head"),
            P("head"),
            P("head"),
            P(),
            P("head", None),
        ),
        out_specs=P("seq", "head"),
        check_vma=False,
    )
```

time: 46.7 us -> 42.7 us (0.914)
  Pallas kernels: 45.7 us -> 41.8 us
    pallas_call x1, Pallas kernels: 45.7 us -> 41.8 us  [on_device(): pl.pallas_call(functools.partial(layer_kernel, seqs, n, heads), out_shape...]
where the time goes in v1:
time: 42.7 us; the launch traced here: 42.6 us
  Pallas kernels  41.8 us (98%)
  local copies, waits for them, and re-layouts  0.8 us (2%)
    pallas_call x1, Pallas kernels, on_device(): pl.pallas_call(functools.partial(layer_kernel, seqs, n, heads), out_shape...  41.8 us

profile of v1, /device:TPU:25, one launch (start us, length us, event | category | flops | bytes accessed | tf_op | source)
XLA Modules:
  0.0 42.6 jit_solution(13616057656817182683)
XLA Ops:
  0.0 41.8 %shard_map.127 = bf16[512,512]{1,0:T(8,128)(2,1)S(1)} custom-call(bf16[512,512]{1,0:T(8,128)(2,1)} %x_ref.1, bf16[2048,256]{1,0:T(8,128)(2,1)} %wq.1, bf16[2048,256]{1,0:T(8,128)(2,1)} %wk.1, bf16[2048,256]{1,0:T(8,128)(2,1)} %wv.1, bf16[2048,256]{1,0:T(8,128)(2,1)} %wg.1, bf16[2,2048]{1,0:T(2,128)(2,1)} %bitcast.5, bf16[2,2048]{1,0:T(2,128)(2,1)} %bitcast.6, ...), custom_call_target="tpu_custom_call" | custom-call | tf_op jit(solution)/shard_map/pallas_call | solution.py:749
  41.8 0.8 %copy.15 = bf16[512,512]{1,0:T(8,128)(2,1)} copy(bf16[512,512]{1,0:T(8,128)(2,1)S(1)} %shard_map.127) | data formatting | bytes 1048576

commit v2 on v1

--- a/solution.py
+++ b/solution.py
@@ -93,7 +93,7 @@
     out_ref,
     w_all, w_flat, spread, x_own, buf, prior, raw, local, reader,
     slab_a, slab_c, mate_a, mate_c, go_a, go_c, in_a, in_c, pre_a, pre_c,
-    w_buf, hid,
+    w_buf, hid, acc,
     beta_ref, step_ref, taps, gain, rates, beta_bias, decay_bias,
     load_sem, small_sem, x_sem, x_send, x_recv, p_send, p_recv, own_sem, w_send, w_recv,
     v_send, v_recv, sa_send, sa_recv, sc_send, sc_recv, side_send, a_send, a_recv, c_send, c_recv,
@@ -117,8 +117,8 @@
     own_load = pltpu.make_async_copy(x_ref, x_own, x_sem)
     own_load.start()
     loads = []
-    for i, (w, at) in enumerate(((wk, 0), (wv, width), (wq, q_at), (wg, g_at))):
-        loads.append(pltpu.make_async_copy(w, w_all.at[:, pl.ds(at, width)], load_sem.at[i]))
+    for w, at in ((wk, 0), (wv, width), (wq, q_at), (wg, g_at)):
+        loads.append(pltpu.make_async_copy(w, w_all.at[:, pl.ds(at, width)], load_sem))
     smalls = [
         pltpu.make_async_copy(source, target, small_sem.at[i])
         for i, (source, target) in enumerate((
@@ -156,20 +156,29 @@
     meet(peers)
     own_load.wait()
 
+    forwards = [m for m in range(1, n) if low_bit(m) > 1]
+    lasts = [m for m in range(1, n) if low_bit(m) == 1]
+
+    def slot_of(m, c):
+        if m in forwards:
+            return forwards.index(m) * pieces + c
+        return len(forwards) * pieces + lasts.index(m) * blocks + c // per_block
+
     def hop(m, bit, c):
         piece = pl.ds(c * PIECE, PIECE)
         source = x_own.at[piece] if m == 0 else buf.at[m, piece]
         got = m | bit
         return remote(
-            source, buf.at[got, piece], x_send.at[got, c], x_recv.at[got, c], (seq, me ^ bit)
+            source, buf.at[got, piece], x_send.at[got - 1], x_recv.at[slot_of(got, c)],
+            (seq, me ^ bit),
         )
 
     tails = [
         remote(
             x_own.at[pl.ds(tokens - PRIOR, PRIOR)],
             prior.at[m],
-            p_send.at[m],
-            p_recv.at[m],
+            p_send,
+            p_recv,
             (seq + 1, me ^ m),
         )
         for m in range(n)
@@ -199,19 +208,29 @@
     for i in range(w_flat.shape[1] // LANES):
         piece = pl.ds(i * LANES, LANES)
         w_all[piece, pl.ds(2 * width, LANES)] = w_flat[:, piece].T.astype(BF16)
-    for load in loads:
-        load.wait()
+    flat = w_all.at[:, pl.ds(0, len(loads) * width)]
+    pltpu.make_async_copy(flat, flat, load_sem).wait()
 
     def weights_of(m, cols):
         start = pl.multiple_of((me ^ m) * feats, LANES)
         return w_all[pl.ds(start, feats), cols]
 
-    def arrive(m, c):
-        hops[m, c].wait_recv()
-        for bit in bits:
-            if bit < low_bit(m):
-                hops[m | bit, c] = hop(m, bit, c)
-                hops[m | bit, c].start()
+    def whole_block(m, b):
+        return buf.at[m, pl.ds(b * BLOCK, BLOCK)]
+
+    def arrive(m, b):
+        if m in lasts:
+            here = whole_block(m, b)
+            remote(
+                here, here, x_send.at[m - 1], x_recv.at[slot_of(m, b * per_block)], (seq, me ^ 1)
+            ).wait_recv()
+            return
+        for c in range(b * per_block, (b + 1) * per_block):
+            hops[m, c].wait_recv()
+            for bit in bits:
+                if bit < low_bit(m):
+                    hops[m | bit, c] = hop(m, bit, c)
+                    hops[m | bit, c].start()
 
     every = pl.ds(0, total_width)
     first_cols = pl.ds(0, main)
@@ -235,8 +254,8 @@
         add([0], at, step, every)
     for at in range(0, tokens, step):
         for m in near:
-            for c in range(at // PIECE, (at + step) // PIECE):
-                arrive(m, c)
+            for b in range(at // BLOCK, (at + step) // BLOCK):
+                arrive(m, b)
             add([m], at, step, every)
 
     within = row >= col
@@ -267,8 +286,8 @@
         @pl.when(has_before)
         def _():
             total = jnp.zeros((PRIOR, total_width), F32)
+            remote(prior, prior, p_send, p_recv, (seq - 1, me)).wait_recv()
             for m in range(n):
-                tails[m].wait_recv()
                 total = total + jnp.dot(prior[m], weights_of(m, every), preferred_element_type=F32)
             raw[pl.ds(0, PRIOR), :] = total
 
@@ -436,16 +455,21 @@
         else:
             source, target = w_ref.at[part_of(odd), columns_of(m)], w_buf.at[m, part_of(odd)]
             passes[m] = remote(
-                w_buf.at[m, part_of(odd)], w_buf.at[m, part_of(odd)], v_send.at[m], v_recv.at[m],
-                (mate, me),
+                w_buf.at[m, part_of(odd)], w_buf.at[m, part_of(odd)], v_send, v_recv, (mate, me)
             )
-        moves[m] = remote(source, target, w_send.at[m], w_recv.at[m], (seq, me ^ m))
+        moves[m] = remote(
+            source, target, w_send, w_recv.at[0 if m in near else 1], (seq, me ^ m)
+        )
+    half_slots = w_buf.at[pl.ds(0, len(passes) // 2)]
+    all_halves = remote(half_slots, half_slots, v_send, v_recv, (mate, me))
+    far_halves = remote(half_slots, half_slots, w_send, w_recv.at[1], (seq, me ^ n // 2))
+    all_slots = w_buf.at[pl.ds(0, len(passes) // 2 + len(near))]
+    all_moves = remote(all_slots, all_slots, w_send, w_recv.at[0], (seq, me ^ 1))
 
     def arrive_block(b):
-        for c in range(b * per_block, (b + 1) * per_block):
-            for m in far:
-                if low_bit(m) > 1:
-                    arrive(m, c)
+        for m in far:
+            if low_bit(m) > 1:
+                arrive(m, b)
 
     direct = [m for m in far if low_bit(m) > 1]
     passed = [m for m in far if low_bit(m) == 1]
@@ -456,8 +480,7 @@
     add(direct, 0, BLOCK, first_cols)
     for b in range(blocks):
         for m in passed:
-            for c in range(b * per_block, (b + 1) * per_block):
-                arrive(m, c)
+            arrive(m, b)
         add(passed, b * BLOCK, BLOCK, first_cols)
 
         def midway():
@@ -516,8 +539,8 @@
 
     def total_copy(source, target, send_sem, recv_sem, r, h, j):
         return remote(
-            source.at[r, h], target.at[r, h], send_sem.at[r, h, j], recv_sem.at[r, h],
-            (seq + 2 + 2 * j, me),
+            source.at[r, h], target.at[r, h], send_sem.at[rounds[r] // 2 - 1 + j, h],
+            recv_sem.at[r, h], (seq + 2 + 2 * j, me),
         )
 
     totals_c, totals_a = {}, {}
@@ -525,9 +548,10 @@
         for h in range(heads):
             for j in range(half // 2):
                 totals_c[r, h, j] = total_copy(go_c, in_c, c_send, c_recv, r, h, j)
-                totals_a[r, h, j] = total_copy(go_a, in_a, a_send, a_recv, r, h, j)
+                if r + 1 < len(rounds):
+                    totals_a[r, h, j] = total_copy(go_a, in_a, a_send, a_recv, r, h, j)
     asides = {
-        h: remote(go_c.at[0, h], in_c.at[0, h], side_send.at[h], c_recv.at[0, h], (seq + 1, me))
+        h: remote(go_c.at[0, h], in_c.at[0, h], side_send.at[h - lone], c_recv.at[0, h], (seq + 1, me))
         for h in range(lone, heads) if rounds
     }
     pair_a, pair_c, firsts = [], [], []
@@ -543,6 +567,9 @@
             for j in reversed(range(rounds[r] // 2)):
                 totals_c[r, h, j].start()
 
+            if r + 1 == len(rounds):
+                return
+
             @pl.when(whole[r])
             def _():
                 total = pair_a[h] if r == 0 else dot(pair_a[h], pre_a[h])
@@ -571,6 +598,9 @@
             def _():
                 pre_c[h] = dot(pre_a[h], in_c[r, h]) + pre_c[h]
 
+            if r + 1 == len(rounds):
+                return
+
             @pl.when(whole[r])
             def _():
                 totals_a[r, h, 0].wait_recv()
@@ -584,17 +614,22 @@
                     pre_a[h] = dot(pre_a[h], in_a[r, h])
 
     def hand_over():
+        far_halves.wait_recv()
         for m in passes:
-            moves[m].wait_recv()
             passes[m].start()
 
     lifts = {}
+
+    def lift_slot(m, h, b):
+        if m in forwards:
+            return (forwards.index(m) * blocks + b) * heads + h
+        return (len(forwards) * heads + lasts.index(m)) * blocks + b
 
     def lift(m, bit, h, b):
         got = m | bit
         return remote(
-            hid.at[m, h, b], hid.at[got, h, b],
-            h_send.at[got, h, b], h_recv.at[got, h, b], (seq, me ^ bit),
+            hid.at[m, b, h], hid.at[got, b, h],
+            h_send.at[got - 1], h_recv.at[lift_slot(got, h, b)], (seq, me ^ bit),
         )
 
     def forward(m, h, b):
@@ -612,7 +647,7 @@
         scaled = head_out * lax.rsqrt(
             jnp.mean(head_out * head_out, axis=-1, keepdims=True) + norm_floor
         )
-        hid[0, h, b] = (scaled * gate).astype(BF16)
+        hid[0, b, h] = (scaled * gate).astype(BF16)
         forward(0, h, b)
 
     for h in range(heads):
@@ -643,52 +678,73 @@
     def _():
         hand_over()
 
-    for r in range(len(rounds) - 1):
-        for h in range(heads):
+    def relay(h):
+        for r in range(len(rounds) - 1):
             take_total(r, h)
             send_total(r + 1, h)
 
+    relay(0)
     for h in range(heads):
+        if h == 0:
+
+            @pl.when(jnp.logical_not(upper))
+            def _():
+                for other in range(1, heads):
+                    relay(other)
+                hand_over()
+
+        else:
+
+            @pl.when(upper)
+            def _():
+                relay(h)
+
         if rounds:
             take_total(len(rounds) - 1, h)
         first_a, first_c = firsts[h]
         state = pre_c[h]
         states.append(jnp.where(is_odd, dot(first_a, state) + first_c, state))
-        if h + 1 < heads:
-            for b in range(blocks // 2):
-                read(h, b)
-
-    @pl.when(jnp.logical_not(upper))
-    def _():
-        hand_over()
-
-    for b in range(blocks):
-        for h in range(heads):
-            if h + 1 == heads or b >= blocks // 2:
-                read(h, b)
+        for b in range(blocks):
+            read(h, b)
 
     own.wait()
     for m in near:
         moves[m].wait_recv()
-    order = sorted(range(1, n), key=lambda m: (m != 1, -low_bit(m), m))
 
     def rows_of(m, b):
-        return jnp.concatenate([hid[m, h, b] for h in range(heads)], axis=1)
-
-    for b in range(blocks):
-        total = jnp.dot(rows_of(0, b), w_buf[0], preferred_element_type=F32)
-        for m in order:
-            if b == 0 and m in passes:
-                passes[m].wait_recv()
-            for h in range(heads):
+        return jnp.concatenate([hid[m, b, h] for h in range(heads)], axis=1)
+
+    def settle(m, b):
+        here = hid.at[m, b]
+        remote(
+            here, here, h_send.at[m - 1], h_recv.at[lift_slot(m, 0, b)], (seq, me ^ 1)
+        ).wait_recv()
+
+    for h in range(heads):
+        for b in range(blocks):
+            for m in forwards:
                 lifts[m, h, b].wait_recv()
                 forward(m, h, b)
+            if h + 1 == heads:
+                total = jnp.dot(rows_of(0, b), w_buf[0], preferred_element_type=F32)
+                for m in near:
+                    settle(m, b)
+                    total = total + jnp.dot(rows_of(m, b), w_buf[m], preferred_element_type=F32)
+                acc[b] = total
+    all_halves.wait_recv()
+    for b in range(blocks):
+        total = acc[b]
+        for m in far:
+            if m in lasts:
+                settle(m, b)
             total = total + jnp.dot(rows_of(m, b), w_buf[m], preferred_element_type=F32)
         out_ref[pl.ds(b * BLOCK, BLOCK), :] = total.astype(BF16)
 
-    for copies in (hops, lifts, moves, passes):
-        for copy in copies.values():
-            copy.wait_send()
+    for m in range(1, n):
+        remote(buf.at[m], buf.at[m], x_send.at[m - 1], x_recv.at[0], (seq, me ^ 1)).wait_send()
+        remote(hid.at[m], hid.at[m], h_send.at[m - 1], h_recv.at[0], (seq, me ^ 1)).wait_send()
+    all_moves.wait_send()
+    all_halves.wait_send()
 
     for h in range(heads):
 
@@ -712,6 +768,9 @@
             def _():
                 for j in range(half // 2):
                     totals_c[r, h, j].wait_send()
+
+                if r + 1 == len(rounds):
+                    return
 
                 @pl.when(whole[r])
                 def _():
@@ -720,8 +779,7 @@
 
     @pl.when(has_next)
     def _():
-        for tail in tails:
-            tail.wait_send()
+        remote(prior, prior, p_send, p_recv, (seq + 1, me)).wait_send()
 
 
 def on_device(
@@ -734,7 +792,8 @@
     heads = beta_weight.shape[1]
     dim = width // heads
     blocks = tokens // BLOCK
-    pieces = tokens // PIECE
+    per_block = BLOCK // PIECE
+    ways = (n // 2 - 1) * blocks
     total_width = 4 * width + LANES
     columns = out_weight.shape[1] // n
     vmem = pl.BlockSpec(memory_space=pltpu.VMEM)
@@ -765,7 +824,8 @@
             stage, stage, stage, stage,
             total, total,
             pltpu.VMEM((n, width, columns), BF16),
-            pltpu.VMEM((n, heads, blocks, BLOCK, dim), BF16),
+            pltpu.VMEM((n, blocks, heads, BLOCK, dim), BF16),
+            pltpu.VMEM((blocks, BLOCK, columns), F32),
             pltpu.VMEM((heads, model), BF16),
             pltpu.VMEM((heads, model), BF16),
             pltpu.VMEM((conv_weight.shape[1], conv_weight.shape[0], width), F32),
@@ -773,29 +833,29 @@
             pltpu.SMEM((heads,), F32),
             pltpu.SMEM((heads,), F32),
             pltpu.SMEM((heads,), F32),
-            dma((4,)),
+            dma(()),
             dma((7,)),
             dma(()),
-            dma((n, pieces)),
-            dma((n, pieces)),
-            dma((n,)),
-            dma((n,)),
+            dma((n - 1,)),
+            dma((ways * per_block + n // 2 * blocks,)),
             dma(()),
-            dma((n,)),
-            dma((n,)),
-            dma((n,)),
-            dma((n,)),
+            dma(()),
+            dma(()),
+            dma(()),
+            dma((2,)),
+            dma(()),
+            dma(()),
             dma((heads,)),
             dma((heads,)),
             dma((heads,)),
             dma((heads,)),
-            dma((heads,)),
-            dma((steps, heads, most)),
+            dma((heads - heads // 2,)),
+            dma((max(1, seqs // 4 - 1), heads)),
+            dma((max(1, steps - 1), heads)),
+            dma((max(1, seqs // 2 - 1), heads)),
             dma((steps, heads)),
-            dma((steps, heads, most)),
-            dma((steps, heads)),
-            dma((n, heads, blocks)),
-            dma((n, heads, blocks)),
+            dma((n - 1,)),
+            dma((ways * heads + n // 2 * blocks,)),
         ],
         compiler_params=pltpu.CompilerParams(
             collective_id=0, has_side_effects=True, vmem_limit_bytes=60 * 1024 * 1024

time: 42.7 us -> 38.4 us (0.90)
  Pallas kernels: 41.8 us -> 37.5 us
    pallas_call x1, Pallas kernels: 41.8 us -> 37.5 us  [on_device(): pl.pallas_call(functools.partial(layer_kernel, seqs, n, heads), out_shape...]
where the time goes in v2:
time: 38.4 us; the launch traced here: 38.3 us
  Pallas kernels  37.5 us (98%)
  local copies, waits for them, and re-layouts  0.8 us (2%)
    pallas_call x1, Pallas kernels, on_device(): pl.pallas_call(functools.partial(layer_kernel, seqs, n, heads), out_shape...  37.5 us
    unnamed x1, local copies, waits for them, and re-layouts  0.8 us

profile of v2, /device:TPU:25, one launch (start us, length us, event | category | flops | bytes accessed | tf_op | source)
XLA Modules:
  0.0 38.3 jit_solution(14301129953742300110)
XLA Ops:
  0.0 37.5 %shard_map.127 = bf16[512,512]{1,0:T(8,128)(2,1)S(1)} custom-call(bf16[512,512]{1,0:T(8,128)(2,1)} %x_ref.1, bf16[2048,256]{1,0:T(8,128)(2,1)} %wq.1, bf16[2048,256]{1,0:T(8,128)(2,1)} %wk.1, bf16[2048,256]{1,0:T(8,128)(2,1)} %wv.1, bf16[2048,256]{1,0:T(8,128)(2,1)} %wg.1, bf16[2,2048]{1,0:T(2,128)(2,1)} %bitcast.5, bf16[2,2048]{1,0:T(2,128)(2,1)} %bitcast.6, ...), custom_call_target="tpu_custom_call" | custom-call | tf_op jit(solution)/shard_map/pallas_call | solution.py:808
  37.5 0.8 %copy.15 = bf16[512,512]{1,0:T(8,128)(2,1)} copy(bf16[512,512]{1,0:T(8,128)(2,1)S(1)} %shard_map.127) | data formatting | bytes 1048576

commit v3 on v2

--- a/solution.py
+++ b/solution.py
@@ -12,6 +12,8 @@
 LANES = 128
 PIECE = 64
 BASE = 8
+
+LAG = 2
 MESH = pl.DeviceIdType.MESH
 F32 = jnp.float32
 BF16 = jnp.bfloat16
@@ -91,11 +93,11 @@
     seqs, n, heads,
     x_ref, wq, wk, wv, wg, beta_in, step_in, taps_in, rates_in, bias_in, shift_in, gain_in, w_ref,
     out_ref,
-    w_all, w_flat, spread, x_own, buf, prior, raw, local, reader,
+    w_all, w_flat, spread, x_own, buf, beside, prior, raw, local, reader,
     slab_a, slab_c, mate_a, mate_c, go_a, go_c, in_a, in_c, pre_a, pre_c,
     w_buf, hid, acc,
     beta_ref, step_ref, taps, gain, rates, beta_bias, decay_bias,
-    load_sem, small_sem, x_sem, x_send, x_recv, p_send, p_recv, own_sem, w_send, w_recv,
+    load_sem, small_sem, x_sem, t_send, t_recv, x_send, x_recv, p_send, p_recv, own_sem, w_send, w_recv,
     v_send, v_recv, sa_send, sa_recv, sc_send, sc_recv, side_send, a_send, a_recv, c_send, c_recv,
     h_send, h_recv,
 ):
@@ -148,8 +150,8 @@
     takes_c = [seq >= 0 if h < lone else seq != 0 for h in range(heads)]
     takes_a = [seq != 1 if h < lone else seq >= 2 for h in range(heads)]
     peers = [(True, (seq, me ^ m)) for m in range(1, n)]
-    peers += [(has_next, (seq + 1, me ^ m)) for m in range(n)]
-    peers += [(has_before, (seq - 1, me ^ m)) for m in range(n)]
+    peers += [(has_next, (seq + 1, me ^ m)) for m in range(2)]
+    peers += [(has_before, (seq - 1, me ^ m)) for m in range(2)]
     for r, half in enumerate(rounds):
         peers += [(sources[r], (seq + 2 + 2 * j, me)) for j in range(half // 2)]
         peers += [(uppers[r], (origins[r], me))]
@@ -173,22 +175,24 @@
             (seq, me ^ bit),
         )
 
-    tails = [
-        remote(
-            x_own.at[pl.ds(tokens - PRIOR, PRIOR)],
-            prior.at[m],
-            p_send,
-            p_recv,
-            (seq + 1, me ^ m),
-        )
-        for m in range(n)
+    own_tail = x_own.at[pl.ds(tokens - PRIOR, PRIOR)]
+    evens = list(range(2, n, 2))
+    crossings = [
+        remote(own_tail, beside.at[i], t_send.at[i], t_recv.at[i], (seq, me ^ m))
+        for i, m in enumerate(evens)
     ]
-
-    @pl.when(has_next)
-    def _():
-        for tail in tails:
-            tail.start()
-
+    for crossing in crossings:
+        crossing.start()
+
+    def send_tail(source, m):
+        @pl.when(has_next)
+        def _():
+            for bit in range(2):
+                remote(
+                    source, prior.at[m | bit], p_send, p_recv, (seq + 1, me ^ bit)
+                ).start()
+
+    send_tail(own_tail, 0)
     hops = {}
     for c in range(pieces):
         for bit in bits:
@@ -252,6 +256,11 @@
     step = 2 * BLOCK if tokens % (2 * BLOCK) == 0 else BLOCK
     for at in range(0, tokens, step):
         add([0], at, step, every)
+
+    for i, m in enumerate(evens):
+        crossings[i].wait_recv()
+        send_tail(beside.at[i], m)
+
     for at in range(0, tokens, step):
         for m in near:
             for b in range(at // BLOCK, (at + step) // BLOCK):
@@ -650,6 +659,13 @@
         hid[0, b, h] = (scaled * gate).astype(BF16)
         forward(0, h, b)
 
+    upper = uppers[-1] if rounds else seq < 0
+
+    def relay(h):
+        for r in range(len(rounds) - 1):
+            take_total(r, h)
+            send_total(r + 1, h)
+
     for h in range(heads):
         @pl.when(takes_c[h])
         def _():
@@ -672,32 +688,17 @@
         if rounds:
             send_total(0, h)
 
-    upper = uppers[-1] if rounds else seq < 0
-
-    @pl.when(upper)
-    def _():
-        hand_over()
-
-    def relay(h):
-        for r in range(len(rounds) - 1):
-            take_total(r, h)
-            send_total(r + 1, h)
-
-    relay(0)
+        @pl.when(jnp.logical_not(upper))
+        def _():
+            relay(h)
+
+
+    hand_over()
+
     for h in range(heads):
-        if h == 0:
-
-            @pl.when(jnp.logical_not(upper))
-            def _():
-                for other in range(1, heads):
-                    relay(other)
-                hand_over()
-
-        else:
-
-            @pl.when(upper)
-            def _():
-                relay(h)
+        @pl.when(upper)
+        def _():
+            relay(h)
 
         if rounds:
             take_total(len(rounds) - 1, h)
@@ -743,6 +744,8 @@
     for m in range(1, n):
         remote(buf.at[m], buf.at[m], x_send.at[m - 1], x_recv.at[0], (seq, me ^ 1)).wait_send()
         remote(hid.at[m], hid.at[m], h_send.at[m - 1], h_recv.at[0], (seq, me ^ 1)).wait_send()
+    for crossing in crossings:
+        crossing.wait_send()
     all_moves.wait_send()
     all_halves.wait_send()
 
@@ -816,6 +819,7 @@
             pltpu.VMEM((LANES, (BASE - 1) * LANES), BF16),
             pltpu.VMEM((tokens, feats), BF16),
             pltpu.VMEM((n, tokens, feats), BF16),
+            pltpu.VMEM((n // 2 - 1, PRIOR, feats), BF16),
             pltpu.VMEM((n, PRIOR, feats), BF16),
             pltpu.VMEM((PRIOR + tokens, total_width), F32),
             pltpu.VMEM((heads, blocks, BLOCK, dim), F32),
@@ -836,6 +840,8 @@
             dma(()),
             dma((7,)),
             dma(()),
+            dma((n // 2 - 1,)),
+            dma((n // 2 - 1,)),
             dma((n - 1,)),
             dma((ways * per_block + n // 2 * blocks,)),
             dma(()),

time: 38.4 us -> 37.7 us (0.982)
  Pallas kernels: 37.5 us -> 36.6 us
    pallas_call x1, Pallas kernels: 37.5 us -> 36.6 us  [on_device(): pl.pallas_call(functools.partial(layer_kernel, seqs, n, heads), out_shape...]
where the time goes in v3:
time: 37.7 us; the launch traced here: 37.4 us
  Pallas kernels  36.6 us (97%)
  local copies, waits for them, and re-layouts  0.8 us (2%)
    pallas_call x1, Pallas kernels, on_device(): pl.pallas_call(functools.partial(layer_kernel, seqs, n, heads), out_shape...  36.6 us
    unnamed x1, local copies, waits for them, and re-layouts  0.8 us

profile of v3, /device:TPU:25, one launch (start us, length us, event | category | flops | bytes accessed | tf_op | source)
XLA Modules:
  0.0 37.4 jit_solution(14253365334376174966)
XLA Ops:
  0.0 36.6 %shard_map.127 = bf16[512,512]{1,0:T(8,128)(2,1)S(1)} custom-call(bf16[512,512]{1,0:T(8,128)(2,1)} %x_ref.1, bf16[2048,256]{1,0:T(8,128)(2,1)} %wq.1, bf16[2048,256]{1,0:T(8,128)(2,1)} %wk.1, bf16[2048,256]{1,0:T(8,128)(2,1)} %wv.1, bf16[2048,256]{1,0:T(8,128)(2,1)} %wg.1, bf16[2,2048]{1,0:T(2,128)(2,1)} %bitcast.5, bf16[2,2048]{1,0:T(2,128)(2,1)} %bitcast.6, ...), custom_call_target="tpu_custom_call" | custom-call | tf_op jit(solution)/shard_map/pallas_call | solution.py:811
  36.6 0.8 %copy.15 = bf16[512,512]{1,0:T(8,128)(2,1)} copy(bf16[512,512]{1,0:T(8,128)(2,1)S(1)} %shard_map.127) | data formatting | bytes 1048576

commit v4 on v3

--- a/solution.py
+++ b/solution.py
@@ -10,7 +10,7 @@
 BLOCK = 128
 PRIOR = 8
 LANES = 128
-PIECE = 64
+PIECE = 128
 BASE = 8
 
 LAG = 2

time: 37.7 us -> 37.5 us (level)
  no operation moved by 1% of the time
where the time goes in v4:
time: 37.5 us; the launch traced here: 37.2 us
  Pallas kernels  36.4 us (97%)
  local copies, waits for them, and re-layouts  0.8 us (2%)
    pallas_call x1, Pallas kernels, on_device(): pl.pallas_call(functools.partial(layer_kernel, seqs, n, heads), out_shape...  36.4 us
    unnamed x1, local copies, waits for them, and re-layouts  0.8 us

profile of v4, /device:TPU:25, one launch (start us, length us, event | category | flops | bytes accessed | tf_op | source)
XLA Modules:
  0.0 37.2 jit_solution(981750540776632920)
XLA Ops:
  0.0 36.4 %shard_map.127 = bf16[512,512]{1,0:T(8,128)(2,1)S(1)} custom-call(bf16[512,512]{1,0:T(8,128)(2,1)} %x_ref.1, bf16[2048,256]{1,0:T(8,128)(2,1)} %wq.1, bf16[2048,256]{1,0:T(8,128)(2,1)} %wk.1, bf16[2048,256]{1,0:T(8,128)(2,1)} %wv.1, bf16[2048,256]{1,0:T(8,128)(2,1)} %wg.1, bf16[2,2048]{1,0:T(2,128)(2,1)} %bitcast.5, bf16[2,2048]{1,0:T(2,128)(2,1)} %bitcast.6, ...), custom_call_target="tpu_custom_call" | custom-call | tf_op jit(solution)/shard_map/pallas_call | solution.py:811
  36.4 0.8 %copy.15 = bf16[512,512]{1,0:T(8,128)(2,1)} copy(bf16[512,512]{1,0:T(8,128)(2,1)S(1)} %shard_map.127) | data formatting | bytes 1048576
